TPU v7x, 32 devices: a whole 2x2x4 slice. The times are simulated.
32 devices in a mesh: dp: 4 (over y, x), expert: 8 (over z, core).
Axes of the slice: x: 2, y: 2, z: 4, core: 2. Of those that a mesh axis runs over, the one named last changes fastest.
Arguments:
- hidden: bfloat16 [8, 4608, 1408], P('expert', 'dp')
- upstream: bfloat16 [8, 4608, 2048], P('expert', 'dp')
- token_counts: int32 [8, 4], P('expert', 'dp'), may hold values from 1 to 1152, as said below
- master: float32 [8, 1408, 2048], P('expert', 'dp'), may hold values from -0.15625 to 0.15625
- first_moment: float32 [8, 1408, 2048], P('expert', 'dp'), may hold values from -6 to 6
- second_moment: float32 [8, 1408, 2048], P('expert', 'dp'), may hold values from 0.25 to 4
- router_input: bfloat16 [4096, 2048], P(('dp', 'expert')), may hold values from -6 to 6
- router_cot: bfloat16 [64, 4096], P(None, ('dp', 'expert'))
- router_master: float32 [64, 2048], replicated, may hold values from -0.125 to 0.125
- router_first: float32 [64, 2048], replicated, may hold values from -6 to 6
- router_second: float32 [64, 2048], replicated, may hold values from 0.25 to 4
- partner: int32 [8], replicated, may hold values from 0 to 7, as said below
Outputs:
- new_weight: bfloat16 [8, 1408, 2048], P('expert')
- new_master: float32 [8, 1408, 2048], P('expert', 'dp')
- new_first: float32 [8, 1408, 2048], P('expert', 'dp')
- new_second: float32 [8, 1408, 2048], P('expert', 'dp')
- router_master_new: float32 [64, 2048], replicated
- router_first_new: float32 [64, 2048], replicated
- router_second_new: float32 [64, 2048], replicated
Inputs may be any that keep to these rules, and one draw needn't show every extreme that they name: partner[partner[p]] = p for every position p; a position with partner[p] = p keeps its expert. The first token_counts[e, d] of replica d's 1152 slots for position e are live, the rest are padding.
All inputs are finite; a program needn't handle non-finite values.
Results may differ from a plain program's by a relative error of at most 0.001.
Values may be sent and summed in bfloat16 or wider, within the bound.
A program may use at most 128 MiB of HBM per device.

v0:
```python
import math
import jax
import jax.numpy as jnp
from jax import lax
from jax.sharding import PartitionSpec as P

beta_first = 0.9
beta_second = 0.95
learn_rate = 0.001
decay_weight = 0.1
adam_eps = 1e-08
norm_eps = 1e-06
correct_first = 1.0 - 0.9**10
correct_second = 1.0 - 0.95**10


def adam_update(gradient, moment_one, moment_two, weights):
    first_new = beta_first * moment_one + (1.0 - beta_first) * gradient
    second_new = beta_second * moment_two + (1.0 - beta_second) * gradient * gradient
    ratio = first_new / correct_first / (jnp.sqrt(second_new / correct_second) + adam_eps)
    weights_new = weights - learn_rate * (ratio + decay_weight * weights)
    return (weights_new, first_new, second_new)


def split_pieces(matrix, groups):
    return matrix.reshape(matrix.shape[0], groups, matrix.shape[1] // groups)


def relocate_state(states, partner):
    groups = lax.axis_size("expert")
    pieces = tuple((split_pieces(member, groups) for member in states))

    def reorder(received):
        arranged = tuple((jnp.take(member, partner, axis=1) for member in received))
        return lax.all_to_all(arranged, "expert", split_axis=1, concat_axis=1, tiled=True)

    result = reorder(
        (
            lax.all_to_all(pieces[0], "expert", split_axis=1, concat_axis=1, tiled=True),
            lax.all_to_all(pieces[1], "expert", split_axis=1, concat_axis=1, tiled=True),
            lax.all_to_all(pieces[2], "expert", split_axis=1, concat_axis=1, tiled=True),
        )
    )
    return tuple((member.reshape(member.shape[0], -1) for member in result))


def regather(weight_shard):
    return lax.all_gather(weight_shard, "dp", axis=0, tiled=True)


def on_device(
    hidden,
    upstream,
    token_counts,
    master,
    first_moment,
    second_moment,
    router_input,
    router_cot,
    router_master,
    router_first,
    router_second,
    partner,
):
    hidden_units = hidden.shape[2]
    features = upstream.shape[2]
    row_count = hidden.shape[1]
    live_rows = jnp.arange(row_count, dtype=jnp.int32) < token_counts[0, 0]
    activations = hidden[0]
    grads_out = upstream[0]
    masked_out = jnp.where(live_rows[:, None], grads_out, jnp.zeros_like(grads_out))
    router_partial = jnp.dot(router_cot, router_input, preferred_element_type=jnp.float32)
    gradient = lax.psum_scatter(
        lax.dot_general(
            activations, masked_out, (((0,), (0,)), ((), ())), preferred_element_type=jnp.float32
        ),
        "dp",
        scatter_dimension=0,
        tiled=True,
    )
    router_grad, expert_square = lax.psum(
        (router_partial, jnp.sum(gradient * gradient)), ("dp", "expert")
    )
    total_square = expert_square + jnp.sum(router_grad * router_grad)
    clip_limit = 2.0 * math.sqrt(
        float(lax.axis_size("expert") * hidden_units * features + router_cot.shape[0] * features)
    )
    factor = jnp.minimum(1.0, clip_limit / (jnp.sqrt(total_square) + norm_eps))
    master_new, first_new, second_new = adam_update(
        factor * gradient, first_moment[0], second_moment[0], master[0]
    )
    router_outs = adam_update(factor * router_grad, router_first, router_second, router_master)
    moved = relocate_state((master_new, first_new, second_new), partner)
    moved_weight = regather(moved[0].astype(jnp.bfloat16))
    return (
        moved_weight[None],
        moved[0][None],
        moved[1][None],
        moved[2][None],
        router_outs[0],
        router_outs[1],
        router_outs[2],
    )


def solution(mesh):
    in_specs = (
        P("expert", "dp", None),
        P("expert", "dp", None),
        P("expert", "dp"),
        P("expert", "dp", None),
        P("expert", "dp", None),
        P("expert", "dp", None),
        P(("dp", "expert"), None),
        P(None, ("dp", "expert")),
        P(),
        P(),
        P(),
        P(),
    )
    out_specs = (
        P("expert", None, None),
        P("expert", "dp", None),
        P("expert", "dp", None),
        P("expert", "dp", None),
        P(),
        P(),
        P(),
    )
    return jax.shard_map(
        on_device, mesh=mesh, in_specs=in_specs, out_specs=out_specs, check_vma=False
    )
```

profile of v0, /device:TPU:0, one launch (start us, length us, event | category | flops | bytes accessed | tf_op | source)
XLA Modules:
  0.0 716.0 jit_solution(1665810783923439618)
XLA Ops:
  9.9 12.9 %convolution_bitcast_fusion = f32[1408,2048]{0,1:T(8,128)} fusion(bf16[1,1152,2048]{2,1,0:T(8,128)(2,1)} %param.15, pred[1152]{0:T(1024)(128)(4,1)S(1)} %iota_compare_fusion, bf16[1,1152,1408]{2,1,0:T(8,128)(2,1)S(1)} %copy-done), kind=kOutput, calls=%fused_computation.3 | convolution fusion | flops 6646136832 | bytes 19498112 | tf_op jit(solution)/shard_map/dot_general | solution.py:74
  22.8 12.0 %copy.42 = f32[1408,2048]{1,0:T(8,128)} copy(f32[1408,2048]{0,1:T(8,128)} %convolution_bitcast_fusion) | data formatting | bytes 23068672
  37.8 2.3 copy.32
  40.1 3.6 copy.33
  43.8 2.4 copy.34
  46.2 105.0 %reduce-scatter.4.cloned.1.call-done = f32[352,2048]{1,0:T(8,128)} async-done(((f32[1408,2048]{1,0:T(8,128)}), f32[352,2048]{1,0:T(8,128)}) %reduce-scatter.4.cloned.1.call-update) | async-done | bytes 2883600
  151.1 2.3 copy.43
  154.9 58.7 %all-reduce.2.cloned.1.call-done = f32[64,2048]{1,0:T(8,128)} async-done(((f32[64,2048]{1,0:T(8,128)}), f32[64,2048]{1,0:T(8,128)}) %all-reduce.2.cloned.1.call-update) | async-done | bytes 524304 | tf_op jit(solution)/shard_map/psum | solution.py:81
  215.4 39.5 %psum.14 = f32[]{:T(128)} all-reduce(f32[]{:T(128)} %multiply_reduce_fusion), channel_id=1, replica_groups=mesh['dp'=4,'expert'=8] {'dp','expert'}, use_global_device_ids=true, to_apply=%region_2.3 | all-reduce | flops 1 | bytes 8 | tf_op jit(solution)/shard_map/psum | solution.py:81
  256.2 6.9 bitcast_subtract_fusion
  263.1 3.4 copy.35
  266.6 4.7 all-to-all-start
  273.5 63.6 %all-to-all-done = f32[352,8,256]{2,0,1:T(8,128)} async-done(((f32[352,8,256]{2,0,1:T(8,128)}), f32[352,8,256]{2,0,1:T(8,128)}, u32[]{:S(2)}, u32[]{:S(2)}) %all-to-all-start) | async-done | bytes 2883616 | tf_op jit(solution)/shard_map/all_to_all | solution.py:39
  337.1 4.4 all-to-all-start.2
  343.9 63.6 %all-to-all-done.2 = f32[352,8,256]{2,0,1:T(8,128)} async-done(((f32[352,8,256]{2,0,1:T(8,128)}), f32[352,8,256]{2,0,1:T(8,128)}, u32[]{:S(2)}, u32[]{:S(2)}) %all-to-all-start.2) | async-done | bytes 2883616 | tf_op jit(solution)/shard_map/all_to_all | solution.py:40
  407.5 4.6 all-to-all-start.4
  412.1 2.5 gather_fusion
  414.7 4.1 gather_fusion.1
  418.8 59.0 %all-to-all-done.4 = f32[352,8,256]{2,0,1:T(8,128)} async-done(((f32[352,8,256]{2,0,1:T(8,128)}), f32[352,8,256]{2,0,1:T(8,128)}, u32[]{:S(2)}, u32[]{:S(2)}) %all-to-all-start.4) | async-done | bytes 2883616 | tf_op jit(solution)/shard_map/all_to_all | solution.py:41
  477.8 4.1 gather_fusion.2
  481.9 6.0 select_bitcast_fusion
  487.9 68.3 %all_to_all.30 = f32[352,8,256]{2,0,1:T(8,128)S(1)} all-to-all(f32[352,8,256]{2,0,1:T(8,128)S(1)} %get-tuple-element.16), channel_id=1, replica_groups=mesh['dp'=4,'expert'=8] {'expert'}, dimensions={1} | all-to-all | bytes 5767168 | tf_op jit(solution)/shard_map/all_to_all | solution.py:35
  556.3 4.4 all-to-all-start.3
  562.2 64.4 %all-to-all-done.3 = f32[352,8,256]{2,0,1:T(8,128)} async-done(((f32[352,8,256]{2,0,1:T(8,128)}), f32[352,8,256]{2,0,1:T(8,128)}, u32[]{:S(2)}, u32[]{:S(2)}) %all-to-all-start.3) | async-done | bytes 2883616 | tf_op jit(solution)/shard_map/all_to_all | solution.py:35
  626.6 4.5 all-to-all-start.5
  631.1 2.9 multiply_subtract_fusion
  634.0 3.2 copy.37
  637.2 4.2 broadcast_in_dim_reshape.9
  641.4 3.5 copy.39
  646.7 50.3 %all-to-all-done.5 = f32[352,8,256]{2,0,1:T(8,128)} async-done(((f32[352,8,256]{2,0,1:T(8,128)}), f32[352,8,256]{2,0,1:T(8,128)}, u32[]{:S(2)}, u32[]{:S(2)}) %all-to-all-start.5) | async-done | bytes 2883616 | tf_op jit(solution)/shard_map/all_to_all | solution.py:35
  696.9 3.5 copy.41
  702.2 6.3 copy.48
  (36 shorter events, 16.9 us)
Async XLA Ops:
  8.0 1.9 copy-start
  8.0 143.1 %reduce-scatter.4.cloned.1.call-start = ((), (), s32[]{:S(2)}) async-start(), calls=%async_computation.9 | async-start | bytes 14417920
  34.8 0.7 copy-start.6
  34.8 3.0 copy-start.4
  34.8 178.7 %all-reduce.2.cloned.1.call-start = ((), (), s32[]{:S(2)}) async-start(), calls=%async_computation.7 | async-start | bytes 1048576 | tf_op jit(solution)/shard_map/psum | solution.py:81
  40.1 3.6 copy-start.5
  266.6 4.7 copy-start.3
  266.6 70.6 %all-to-all-start = ((f32[352,8,256]{2,0,1:T(8,128)}), f32[352,8,256]{2,0,1:T(8,128)}, u32[]{:S(2)}, u32[]{:S(2)}) async-start(f32[352,8,256]{2,0,1:T(8,128)} %copy.35), calls=%async_computation | async-start | bytes 5767168 | tf_op jit(solution)/shard_map/all_to_all | solution.py:39
  273.5 68.1 %copy-start.2 = (f32[352,2048]{0,1:T(8,128)S(1)}, f32[352,2048]{0,1:T(8,128)}, u32[]{:S(2)}) copy-start(f32[352,2048]{0,1:T(8,128)} %get-tuple-element.13) | copy-start | bytes 8650756
  337.1 70.3 %all-to-all-start.2 = ((f32[352,8,256]{2,0,1:T(8,128)}), f32[352,8,256]{2,0,1:T(8,128)}, u32[]{:S(2)}, u32[]{:S(2)}) async-start(f32[352,8,256]{2,0,1:T(8,128)} %copy.38), calls=%async_computation.2 | async-start | bytes 5767168 | tf_op jit(solution)/shard_map/all_to_all | solution.py:40
  343.9 68.2 %copy-start.7 = (s32[8]{0:T(128)S(1)}, s32[8]{0:T(128)}, u32[]{:S(2)}) copy-start(s32[8]{0:T(128)} %param.25) | copy-start | bytes 100
  407.5 70.3 %all-to-all-start.4 = ((f32[352,8,256]{2,0,1:T(8,128)}), f32[352,8,256]{2,0,1:T(8,128)}, u32[]{:S(2)}, u32[]{:S(2)}) async-start(f32[352,8,256]{2,0,1:T(8,128)} %copy.40), calls=%async_computation.4 | async-start | bytes 5767168 | tf_op jit(solution)/shard_map/all_to_all | solution.py:41
  556.3 70.3 %all-to-all-start.3 = ((f32[352,8,256]{2,0,1:T(8,128)}), f32[352,8,256]{2,0,1:T(8,128)}, u32[]{:S(2)}, u32[]{:S(2)}) async-start(f32[352,8,256]{2,0,1:T(8,128)} %get-tuple-element.15), calls=%async_computation.3 | async-start | bytes 5767168 | tf_op jit(solution)/shard_map/all_to_all | solution.py:35
  560.7 141.6 %all-gather.2.cloned.1.call-start = ((), (), s32[]{:S(2)}) async-start(), calls=%async_computation.8 | async-start | bytes 7208960 | tf_op jit(solution)/shard_map/all_gather | solution.py:48
  626.6 70.4 %all-to-all-start.5 = ((f32[352,8,256]{2,0,1:T(8,128)}), f32[352,8,256]{2,0,1:T(8,128)}, u32[]{:S(2)}, u32[]{:S(2)}) async-start(f32[352,8,256]{2,0,1:T(8,128)} %get-tuple-element.14), calls=%async_computation.5 | async-start | bytes 5767168 | tf_op jit(solution)/shard_map/all_to_all | solution.py:35
  702.2 6.3 copy-start.1
Sparse Core Ops, SparseCore 0:
  35.0 116.1 reduce-scatter.3
  563.9 67.7 all-gather.1
Sparse Core Ops, SparseCore 1:
  41.2 172.3 all-reduce.1
where the time goes:
time: 717 us; the launch traced here: 716 us
  waiting for transfers between devices  465 us (65%)
  blocking collectives  108 us (15%)
  local copies, waits for them, and re-layouts  68.8 us (10%)
  starting transfers between devices  22.7 us (3%)
  other arithmetic  19.2 us (3%)
  between operations  17.8 us (2%)
  matrix products  15.1 us (2%)
    all_to_all x2, waiting for transfers between devices, reorder(): lax.all_to_all(arranged, 'expert', split_axis=1, concat_axis=1, tiled=True)  115 us
    unnamed x4, waiting for transfers between devices  105 us
    all_to_all x1, blocking collectives, reorder(): lax.all_to_all(arranged, 'expert', split_axis=1, concat_axis=1, tiled=True)  68.3 us
    all_to_all x1, waiting for transfers between devices, relocate_state(): lax.all_to_all(pieces[1], 'expert', split_axis=1, concat_axis=1, tiled=True)  63.6 us
    all_to_all x1, waiting for transfers between devices, relocate_state(): lax.all_to_all(pieces[0], 'expert', split_axis=1, concat_axis=1, tiled=True)  63.6 us
    all_to_all x1, waiting for transfers between devices, relocate_state(): lax.all_to_all(pieces[2], 'expert', split_axis=1, concat_axis=1, tiled=True)  59 us
    psum x1, waiting for transfers between devices, on_device(): lax.psum((router_partial, jnp.sum(gradient * gradient)), ('dp', 'expert'))  58.7 us
    psum x1, blocking collectives, on_device(): lax.psum((router_partial, jnp.sum(gradient * gradient)), ('dp', 'expert'))  39.5 us
  transfers between devices with their start and end apart: 8, of which 7 were waited for; matrix products, arithmetic and copies ran while one was open for 7% of the time, Pallas kernels for 0%

commit v1 on v0

--- a/solution.py
+++ b/solution.py
@@ -38,7 +38,15 @@
         (
             lax.all_to_all(pieces[0], "expert", split_axis=1, concat_axis=1, tiled=True),
             lax.all_to_all(pieces[1], "expert", split_axis=1, concat_axis=1, tiled=True),
-            lax.all_to_all(pieces[2], "expert", split_axis=1, concat_axis=1, tiled=True),
+            jnp.concatenate(
+                lax.all_to_all(
+                    jnp.stack(jnp.split(pieces[2], lax.psum(1, axis_name="expert"), 1), 0),
+                    concat_axis=0,
+                    axis_name="expert",
+                    split_axis=0,
+                ),
+                1,
+            ),
         )
     )
     return tuple((member.reshape(member.shape[0], -1) for member in result))

time: 717 us -> 734 us (1.024)
  local copies, waits for them, and re-layouts: 68.8 us -> 82.6 us
    unnamed x22 -> x37, local copies, waits for them, and re-layouts: 30.8 us -> 39 us
  transfers between devices with their start and end apart: 8 -> 8, of which waited for: 7 -> 7; matrix products, arithmetic and copies ran while one was open for 7% -> 8% of each run, Pallas kernels for 0% -> 0%
where the time goes in v1:
time: 734 us; the launch traced here: 733 us
  waiting for transfers between devices  468 us (64%)
  blocking collectives  108 us (15%)
  local copies, waits for them, and re-layouts  82.6 us (11%)
  starting transfers between devices  22.7 us (3%)
  other arithmetic  18.9 us (3%)
  between operations  17.9 us (2%)
  matrix products  15.1 us (2%)
    all_to_all x2, waiting for transfers between devices, reorder(): lax.all_to_all(arranged, 'expert', split_axis=1, concat_axis=1, tiled=True)  118 us
    unnamed x4, waiting for transfers between devices  105 us
    all_to_all x1, blocking collectives, reorder(): lax.all_to_all(arranged, 'expert', split_axis=1, concat_axis=1, tiled=True)  68.3 us
    all_to_all x1, waiting for transfers between devices, relocate_state(): lax.all_to_all(jnp.stack(jnp.split(pieces[2], lax.psum(1, axis_name='expe...  63.6 us
    all_to_all x1, waiting for transfers between devices, relocate_state(): lax.all_to_all(pieces[0], 'expert', split_axis=1, concat_axis=1, tiled=True)  63.4 us
    all_to_all x1, waiting for transfers between devices, relocate_state(): lax.all_to_all(pieces[1], 'expert', split_axis=1, concat_axis=1, tiled=True)  59.2 us
    psum x1, waiting for transfers between devices, on_device(): lax.psum((router_partial, jnp.sum(gradient * gradient)), ('dp', 'expert'))  58.7 us
    psum x1, blocking collectives, on_device(): lax.psum((router_partial, jnp.sum(gradient * gradient)), ('dp', 'expert'))  39.5 us
  transfers between devices with their start and end apart: 8, of which 7 were waited for; matrix products, arithmetic and copies ran while one was open for 8% of the time, Pallas kernels for 0%

profile of v1, /device:TPU:0, one launch (start us, length us, event | category | flops | bytes accessed | tf_op | source)
XLA Modules:
  0.0 733.0 jit_solution(525391761075048116)
XLA Ops:
  9.9 12.9 %convolution_bitcast_fusion = f32[1408,2048]{0,1:T(8,128)} fusion(bf16[1,1152,2048]{2,1,0:T(8,128)(2,1)} %param.15, pred[1152]{0:T(1024)(128)(4,1)S(1)} %iota_compare_fusion, bf16[1,1152,1408]{2,1,0:T(8,128)(2,1)S(1)} %copy-done), kind=kOutput, calls=%fused_computation.3 | convolution fusion | flops 6646136832 | bytes 19498112 | tf_op jit(solution)/shard_map/dot_general | solution.py:82
  22.8 12.0 %copy.56 = f32[1408,2048]{1,0:T(8,128)} copy(f32[1408,2048]{0,1:T(8,128)} %convolution_bitcast_fusion) | data formatting | bytes 23068672
  37.8 2.3 copy.39
  40.1 3.6 copy.40
  43.8 2.4 copy.41
  46.2 105.0 %reduce-scatter.4.cloned.1.call-done = f32[352,2048]{1,0:T(8,128)} async-done(((f32[1408,2048]{1,0:T(8,128)}), f32[352,2048]{1,0:T(8,128)}) %reduce-scatter.4.cloned.1.call-update) | async-done | bytes 2883600
  154.9 58.7 %all-reduce.2.cloned.1.call-done = f32[64,2048]{1,0:T(8,128)} async-done(((f32[64,2048]{1,0:T(8,128)}), f32[64,2048]{1,0:T(8,128)}) %all-reduce.2.cloned.1.call-update) | async-done | bytes 524304 | tf_op jit(solution)/shard_map/psum | solution.py:89
  215.4 39.5 %psum.14 = f32[]{:T(128)} all-reduce(f32[]{:T(128)} %multiply_reduce_fusion), channel_id=1, replica_groups=mesh['dp'=4,'expert'=8] {'dp','expert'}, use_global_device_ids=true, to_apply=%region_2.3 | all-reduce | flops 1 | bytes 8 | tf_op jit(solution)/shard_map/psum | solution.py:89
  256.2 6.6 bitcast_subtract_fusion
  272.2 4.7 all-to-all-start.4
  279.2 63.6 %all-to-all-done.4 = f32[8,352,1,256]{3,1,2,0:T(8,128)} async-done(((f32[8,352,1,256]{3,1,2,0:T(8,128)}), f32[8,352,1,256]{3,1,2,0:T(8,128)}, u32[]{:S(2)}, u32[]{:S(2)}) %all-to-all-start.4) | async-done | bytes 2883616 | tf_op jit(solution)/shard_map/all_to_all | solution.py:42
  342.8 4.6 all-to-all-start
  349.7 63.4 %all-to-all-done = f32[352,8,256]{2,0,1:T(8,128)} async-done(((f32[352,8,256]{2,0,1:T(8,128)}), f32[352,8,256]{2,0,1:T(8,128)}, u32[]{:S(2)}, u32[]{:S(2)}) %all-to-all-start) | async-done | bytes 2883616 | tf_op jit(solution)/shard_map/all_to_all | solution.py:39
  413.1 4.4 all-to-all-start.2
  417.6 2.5 gather_fusion.2
  420.1 4.1 gather_fusion
  424.3 59.2 %all-to-all-done.2 = f32[352,8,256]{2,0,1:T(8,128)} async-done(((f32[352,8,256]{2,0,1:T(8,128)}), f32[352,8,256]{2,0,1:T(8,128)}, u32[]{:S(2)}, u32[]{:S(2)}) %all-to-all-start.2) | async-done | bytes 2883616 | tf_op jit(solution)/shard_map/all_to_all | solution.py:40
  483.4 4.1 gather_fusion.1
  487.5 6.0 select_bitcast_fusion
  493.6 68.3 %all_to_all.30 = f32[352,8,256]{2,0,1:T(8,128)S(1)} all-to-all(f32[352,8,256]{2,0,1:T(8,128)S(1)} %get-tuple-element.24), channel_id=1, replica_groups=mesh['dp'=4,'expert'=8] {'expert'}, dimensions={1} | all-to-all | bytes 5767168 | tf_op jit(solution)/shard_map/all_to_all | solution.py:35
  561.9 4.4 all-to-all-start.3
  567.9 64.3 %all-to-all-done.3 = f32[352,8,256]{2,0,1:T(8,128)} async-done(((f32[352,8,256]{2,0,1:T(8,128)}), f32[352,8,256]{2,0,1:T(8,128)}, u32[]{:S(2)}, u32[]{:S(2)}) %all-to-all-start.3) | async-done | bytes 2883616 | tf_op jit(solution)/shard_map/all_to_all | solution.py:35
  632.2 4.5 all-to-all-start.5
  636.7 2.9 multiply_subtract_fusion
  639.6 5.1 copy.46
  644.7 4.2 broadcast_in_dim_reshape.10
  648.9 53.7 %all-to-all-done.5 = f32[352,8,256]{2,0,1:T(8,128)} async-done(((f32[352,8,256]{2,0,1:T(8,128)}), f32[352,8,256]{2,0,1:T(8,128)}, u32[]{:S(2)}, u32[]{:S(2)}) %all-to-all-start.5) | async-done | bytes 2883616 | tf_op jit(solution)/shard_map/all_to_all | solution.py:35
  702.6 5.1 copy.55
  707.7 4.2 broadcast_in_dim_reshape.11
  711.8 3.2 copy.44
  715.1 4.2 broadcast_in_dim_reshape.9
  719.3 6.3 copy.77
  (52 shorter events, 25.0 us)
Async XLA Ops:
  8.0 1.9 copy-start
  8.0 143.1 %reduce-scatter.4.cloned.1.call-start = ((), (), s32[]{:S(2)}) async-start(), calls=%async_computation.9 | async-start | bytes 14417920
  34.8 0.7 copy-start.6
  34.8 3.0 copy-start.4
  34.9 178.7 %all-reduce.2.cloned.1.call-start = ((), (), s32[]{:S(2)}) async-start(), calls=%async_computation.7 | async-start | bytes 1048576 | tf_op jit(solution)/shard_map/psum | solution.py:89
  40.1 3.6 copy-start.5
  272.2 4.7 copy-start.3
  272.2 70.6 %all-to-all-start.4 = ((f32[8,352,1,256]{3,1,2,0:T(8,128)}), f32[8,352,1,256]{3,1,2,0:T(8,128)}, u32[]{:S(2)}, u32[]{:S(2)}) async-start(f32[8,352,1,256]{3,1,2,0:T(8,128)} %bitcast_dynamic-update-slice_fusion), calls=%async_computation.4 | async-start | bytes 5767168 | tf_op jit(solution)/shard_map/all_to_all | solution.py:42
  279.2 68.2 %copy-start.2 = (f32[352,2048]{0,1:T(8,128)S(1)}, f32[352,2048]{0,1:T(8,128)}, u32[]{:S(2)}) copy-start(f32[352,2048]{0,1:T(8,128)} %get-tuple-element.12) | copy-start | bytes 8650756
  342.8 70.3 %all-to-all-start = ((f32[352,8,256]{2,0,1:T(8,128)}), f32[352,8,256]{2,0,1:T(8,128)}, u32[]{:S(2)}, u32[]{:S(2)}) async-start(f32[352,8,256]{2,0,1:T(8,128)} %copy.42), calls=%async_computation | async-start | bytes 5767168 | tf_op jit(solution)/shard_map/all_to_all | solution.py:39
  349.7 67.9 %copy-start.7 = (s32[8]{0:T(128)S(1)}, s32[8]{0:T(128)}, u32[]{:S(2)}) copy-start(s32[8]{0:T(128)} %param.25) | copy-start | bytes 100
  413.1 70.3 %all-to-all-start.2 = ((f32[352,8,256]{2,0,1:T(8,128)}), f32[352,8,256]{2,0,1:T(8,128)}, u32[]{:S(2)}, u32[]{:S(2)}) async-start(f32[352,8,256]{2,0,1:T(8,128)} %copy.45), calls=%async_computation.2 | async-start | bytes 5767168 | tf_op jit(solution)/shard_map/all_to_all | solution.py:40
  561.9 70.3 %all-to-all-start.3 = ((f32[352,8,256]{2,0,1:T(8,128)}), f32[352,8,256]{2,0,1:T(8,128)}, u32[]{:S(2)}, u32[]{:S(2)}) async-start(f32[352,8,256]{2,0,1:T(8,128)} %get-tuple-element.23), calls=%async_computation.3 | async-start | bytes 5767168 | tf_op jit(solution)/shard_map/all_to_all | solution.py:35
  566.3 152.9 %all-gather.2.cloned.1.call-start = ((), (), s32[]{:S(2)}) async-start(), calls=%async_computation.8 | async-start | bytes 7208960 | tf_op jit(solution)/shard_map/all_gather | solution.py:56
  632.2 70.4 %all-to-all-start.5 = ((f32[352,8,256]{2,0,1:T(8,128)}), f32[352,8,256]{2,0,1:T(8,128)}, u32[]{:S(2)}, u32[]{:S(2)}) async-start(f32[352,8,256]{2,0,1:T(8,128)} %get-tuple-element.22), calls=%async_computation.5 | async-start | bytes 5767168 | tf_op jit(solution)/shard_map/all_to_all | solution.py:35
  719.3 6.3 copy-start.1
Sparse Core Ops, SparseCore 0:
  35.0 116.1 reduce-scatter.3
  569.0 67.8 all-gather.1
Sparse Core Ops, SparseCore 1:
  41.2 172.3 all-reduce.1
